TPU v7x, 256 devices: a whole 4x4x8 slice. The times are simulated.
256 devices in a mesh: expert: 16 (over x, y), tensor: 8 (over z), replica: 2 (over core).
Axes of the slice: x: 4, y: 4, z: 8, core: 2. Of those that a mesh axis runs over, the one named last changes fastest.
Arguments:
- trained: float32 [16, 7168, 2048], P('replica', 'tensor', 'expert'), may hold values from -3080 to 3080
- snapshot: bfloat16 [16, 7168, 2048], P('replica', 'tensor', 'expert'), may hold values from -3072 to 3072
- changed: int32 [16, 56, 16], P('replica', 'tensor', 'expert'), may hold values from 0 to 1, as said below
- placement: int32 [16], replicated, may hold values from 0 to 15, each once
Outputs:
- rotated_update: bfloat16 [16, 7168, 2048], P('expert', None, 'tensor')
Inputs may be any that keep to these rules, and one draw needn't show every extreme that they name: `placement`: each of the 16 experts appears exactly once. `changed`: in each aligned block of 7 block rows by 1 block columns of one expert, at most 4 entries are 1; for every expert some such block has exactly 4.
All inputs are finite; a program needn't handle non-finite values.
Results may differ from a plain program's by a relative error of at most 0.001.
Values may be sent and summed in bfloat16 or wider, within the bound.
A program may use at most 64 MiB of HBM per device.

v0:
```python
import math
import jax
import jax.numpy as jnp
from jax import lax
from jax.sharding import PartitionSpec as P

BLK = 128


def hadamard():
    positions = jnp.arange(BLK, dtype=jnp.int32)
    parity = jnp.zeros((BLK, BLK), jnp.int32)
    for bit_level in range(BLK.bit_length() - 1):
        parity = parity + (positions[:, None] >> bit_level & 1) * (
            positions[None, :] >> bit_level & 1
        )
    return (1 - 2 * (parity % 2)).astype(jnp.float32) / math.sqrt(BLK)


def body(trained, snapshot, changed, placement):
    hadamard_table = hadamard()
    local_experts, local_rows, local_cols = trained.shape
    copies = lax.axis_size("replica")
    tensor_count = lax.axis_size("tensor")
    expert_count = lax.axis_size("expert")
    members = expert_count // tensor_count
    slot_total = placement.shape[0]
    owner_slots = slot_total // expert_count
    block_rows = local_rows // BLK
    block_cols = local_cols // BLK
    part_rows = BLK // copies
    block_count = block_rows * block_cols
    capacity = (4 * block_count + 3) // 7
    block_flags = changed.reshape(local_experts, block_count)
    position = jnp.arange(block_count, dtype=jnp.int32)
    ranking = jnp.where(block_flags == 1, position[None, :], block_count + position[None, :])
    picked = jnp.argsort(ranking, axis=1)[:, :capacity]
    used_slots = jnp.take_along_axis(block_flags, picked, axis=1)
    expert_ids = jnp.arange(local_experts, dtype=jnp.int32)[:, None]
    row_ids = picked // block_cols
    col_ids = picked % block_cols
    new_tiles = trained.reshape(local_experts, block_rows, BLK, block_cols, BLK)[
        expert_ids, row_ids, :, col_ids, :
    ]
    old_tiles = snapshot.reshape(local_experts, block_rows, BLK, block_cols, BLK)[
        expert_ids, row_ids, :, col_ids, :
    ]
    delta_tiles = jnp.where(
        used_slots[:, :, None, None] == 1, new_tiles - old_tiles.astype(jnp.float32), 0.0
    )
    coded_tiles = jnp.einsum(
        "ij,pmjk->pmik", hadamard_table, delta_tiles, precision=lax.Precision.HIGHEST
    ).astype(jnp.bfloat16)
    coded_tiles = coded_tiles.reshape(local_experts, capacity, copies, part_rows, BLK)
    spots_pair = jnp.broadcast_to(picked[:, :, None], (local_experts, capacity, copies))
    tiles_all, spots_all = (
        lax.all_to_all(coded_tiles, "replica", split_axis=2, concat_axis=0, tiled=True),
        lax.all_to_all(spots_pair, "replica", split_axis=2, concat_axis=0, tiled=True),
    )
    chosen = jnp.take(tiles_all, placement, axis=0).reshape(
        slot_total, 1, 1, capacity, part_rows, BLK
    )
    chosen_spots = jnp.take(spots_all, placement, axis=0).reshape(slot_total, 1, 1, capacity)
    tiles_in, spot_numbers = (
        lax.all_to_all(
            lax.all_to_all(chosen, "expert", split_axis=0, concat_axis=2, tiled=True),
            "tensor",
            split_axis=2,
            concat_axis=1,
            tiled=True,
        ),
        lax.all_to_all(
            lax.all_to_all(chosen_spots, "expert", split_axis=0, concat_axis=2, tiled=True),
            "tensor",
            split_axis=2,
            concat_axis=1,
            tiled=True,
        ),
    )
    source_count = tiles_in.shape[1]
    one_hot = (spot_numbers[..., None] == position).astype(jnp.bfloat16)
    placed = jnp.einsum(
        "osnmg,osnmab->osngab", one_hot, tiles_in, preferred_element_type=jnp.float32
    ).astype(jnp.bfloat16)
    placed = placed.reshape(
        owner_slots, source_count, members, block_rows, block_cols, part_rows, BLK
    )
    placed = jnp.transpose(placed, (0, 1, 3, 5, 2, 4, 6))
    owner_cols = members * block_cols * BLK
    owned_rows = placed.reshape(owner_slots, source_count, block_rows, 1, part_rows, owner_cols)
    whole_rows = lax.all_gather(owned_rows, "replica", axis=3, tiled=True)
    return whole_rows.reshape(owner_slots, tensor_count * block_rows * BLK, owner_cols)


def solution(mesh):
    in_specs = (
        P("replica", "tensor", "expert"),
        P("replica", "tensor", "expert"),
        P("replica", "tensor", "expert"),
        P(),
    )
    out_specs = P("expert", None, "tensor")
    return jax.shard_map(body, mesh=mesh, in_specs=in_specs, out_specs=out_specs, check_vma=False)
```

profile of v0, /device:TPU:1, one launch (start us, length us, event | category | flops | bytes accessed | tf_op | source)
XLA Modules:
  0.0 145.1 jit_solution(11660733728816668597)
XLA Ops:
  6.5 0.9 iota_select_fusion
  7.4 0.7 sort.17
  8.1 0.6 broadcast_in_dim.55
  8.7 6.4 %all-to-all-start = ((s32[8,4,2]{0,1,2:T(4,128)}), s32[8,4,2]{0,1,2:T(4,128)S(1)}, u32[]{:S(2)}, u32[]{:S(2)}) async-start(s32[8,4,2]{0,1,2:T(4,128)} %broadcast_in_dim.55), calls=%async_computation | async-start | bytes 8192 | tf_op jit(solution)/shard_map/all_to_all | solution.py:58
  15.1 0.7 compare_and_fusion
  15.8 0.7 compare_select_fusion.1
  16.4 0.8 copy.38
  17.4 0.7 gather_fusion.4
  18.2 0.1 copy.48
  18.3 0.8 gather_fusion.2
  19.1 4.0 %gather_fusion.1 = f32[32,128,128]{2,1,0:T(8,128)} fusion(f32[8,7,128,1,128]{4,2,1,0,3:T(8,128)} %bitcast.67, s32[32]{0:T(128)S(1)} %reshape.261), kind=kCustom, calls=%fused_computation.1 | custom fusion | bytes 4194688 | tf_op jit(solution)/shard_map/gather | solution.py:42
  23.2 1.9 %convert_subtract_fusion = f32[32,128,128]{2,1,0:T(8,128)S(1)} fusion(f32[32,128,128]{2,1,0:T(8,128)} %gather_fusion.1, bf16[32,128,128]{2,1,0:T(8,128)(2,1)S(1)} %gather_fusion.2), kind=kLoop, calls=%fused_computation.5 | loop fusion | flops 1048576 | bytes 5242880 | tf_op jit(solution)/shard_map/sub | solution.py:49
  25.0 2.3 %fusion.2 = bf16[8,4,128,128]{2,3,1,0:T(8,128)(2,1)S(1)} fusion(f32[8,4,128,128]{3,2,1,0:T(8,128)S(1)} %bitcast.61, pred[8,4]{1,0:T(8,128)(4,1)S(1)} %copy.48, s32[128]{0:T(128)S(1)} %get-tuple-element.7, s32[128]{0:T(128)S(1)} %get-tuple-element.8, s32[128]{0:T(128)S(1)} %get-tuple-element.9, s32[128]{0:T(128)S(1)} %get-tuple-element.10, ...), kind=kOutput, calls=%fused_computation.9 | convolution fusion | flops 806813696 | bytes 3149344 | tf_op jit(solution)/shard_map/ij,pmjk->pmik/dot_general | solution.py:51
  27.3 1.1 copy.49
  28.4 3.6 %all-to-all-start.3 = ((bf16[8,4,2,64,128]{4,3,1,0,2:T(8,128)(2,1)}), bf16[8,4,2,64,128]{4,3,1,0,2:T(8,128)(2,1)S(1)}, u32[]{:S(2)}, u32[]{:S(2)}) async-start(bf16[8,4,2,64,128]{4,3,1,0,2:T(8,128)(2,1)} %copy.49), calls=%async_computation.3 | async-start | bytes 2097152 | tf_op jit(solution)/shard_map/all_to_all | solution.py:57
  32.1 0.6 gather_fusion
  32.7 0.7 copy.43
  33.4 0.3 all-to-all-done.3
  33.7 5.1 %all-to-all-start.1 = ((s32[16,1,1,4]{3,2,1,0:T(1,128)}), s32[16,1,1,4]{3,2,1,0:T(1,128)}, u32[]{:S(2)}, u32[]{:S(2)}) async-start(s32[16,1,1,4]{3,2,1,0:T(1,128)} %copy.43), calls=%async_computation.1 | async-start | bytes 16384 | tf_op jit(solution)/shard_map/all_to_all | solution.py:73
  38.9 2.0 %gather_fusion.3 = bf16[16,4,64,128]{3,2,1,0:T(8,128)(2,1)S(1)} fusion(bf16[16,4,64,128]{3,2,1,0:T(8,128)(2,1)} %bitcast.65, s32[1024]{0:T(1024)S(1)} %pad_clamp_fusion), kind=kCustom, calls=%fused_computation.3 | custom fusion | bytes 2097216 | tf_op jit(solution)/shard_map/jit(_take)/gather | solution.py:60
  40.8 1.1 fusion.5
  42.0 3.2 %all-to-all-done.1 = s32[16,1,1,4]{3,2,1,0:T(1,128)} async-done(((s32[16,1,1,4]{3,2,1,0:T(1,128)}), s32[16,1,1,4]{3,2,1,0:T(1,128)}, u32[]{:S(2)}, u32[]{:S(2)}) %all-to-all-start.1) | async-done | bytes 288 | tf_op jit(solution)/shard_map/all_to_all | solution.py:73
  45.2 18.6 %all_to_all.78 = bf16[16,1,1,4,64,128]{5,4,3,2,1,0:T(8,128)(2,1)S(1)} all-to-all(bf16[16,1,1,4,64,128]{5,4,3,2,1,0:T(8,128)(2,1)} %fusion.5), channel_id=1, replica_groups=mesh['expert'=16,'tensor'=8,'replica'=2] {'expert'}, dimensions={0} | all-to-all | bytes 2097152 | tf_op jit(solution)/shard_map/all_to_all | solution.py:66
  63.8 32.6 %all_to_all.79 = bf16[1,1,16,4,64,128]{5,4,3,1,0,2:T(8,128)(2,1)} all-to-all(bf16[1,1,16,4,64,128]{5,4,3,1,0,2:T(8,128)(2,1)S(1)} %bitcast.66), channel_id=1, replica_groups=mesh['expert'=16,'tensor'=8,'replica'=2] {'tensor'}, dimensions={2} | all-to-all | bytes 2097152 | tf_op jit(solution)/shard_map/all_to_all | solution.py:65
  96.3 4.3 %all-to-all-start.2 = ((s32[1,1,16,4]{3,1,0,2:T(1,128)}), s32[1,1,16,4]{3,1,0,2:T(1,128)S(1)}, u32[]{:S(2)}, u32[]{:S(2)}) async-start(s32[1,1,16,4]{3,1,0,2:T(1,128)} %bitcast.31), calls=%async_computation.2 | async-start | bytes 16384 | tf_op jit(solution)/shard_map/all_to_all | solution.py:72
  100.7 2.1 %copy.52 = bf16[1,1,16,4,64,128]{5,3,4,2,1,0:T(4,128)(2,1)S(1)} copy(bf16[1,1,16,4,64,128]{5,4,3,1,0,2:T(8,128)(2,1)} %all_to_all.79) | data formatting | bytes 2097152 | tf_op jit(solution)/shard_map/all_to_all | solution.py:65
  102.8 4.4 %all-to-all-done.2 = s32[1,1,16,4]{3,1,0,2:T(1,128)S(1)} async-done(((s32[1,1,16,4]{3,1,0,2:T(1,128)}), s32[1,1,16,4]{3,1,0,2:T(1,128)S(1)}, u32[]{:S(2)}, u32[]{:S(2)}) %all-to-all-start.2) | async-done | bytes 288 | tf_op jit(solution)/shard_map/all_to_all | solution.py:72
  107.2 1.3 convert_bitcast_fusion
  108.5 3.3 %copy.53 = bf16[1,8,7,64,2,1,128]{6,4,3,2,1,5,0:T(2,128)(2,1)} copy(bf16[1,8,7,64,2,1,128]{6,2,3,4,1,5,0:T(8,128)(2,1)S(1)} %convert_bitcast_fusion) | data formatting | bytes 3670016 | tf_op jit(solution)/shard_map/transpose | solution.py:88
  111.8 5.3 %reshape.227 = bf16[1,8,7,1,64,256]{5,4,2,1,3,0:T(8,128)(2,1)} reshape(bf16[1,8,7,64,2,1,128]{6,4,3,2,1,5,0:T(2,128)(2,1)} %copy.53) | data formatting | bytes 3670016 | tf_op jit(solution)/shard_map/reshape | solution.py:90
  117.1 16.8 %all-gather.2.cloned.1.call-done = bf16[1,8,7,2,64,256]{5,4,2,1,0,3:T(8,128)(2,1)} async-done(((bf16[1,8,7,1,64,256]{5,4,2,1,0,3:T(8,128)(2,1)}), bf16[1,8,7,2,64,256]{5,4,2,1,0,3:T(8,128)(2,1)}) %all-gather.2.cloned.1.call-update) | async-done | bytes 3670032 | tf_op jit(solution)/shard_map/all_gather | solution.py:91
  133.9 4.4 %copy.55 = bf16[1,8,7,2,64,256]{5,4,3,2,1,0:T(8,128)(2,1)} copy(bf16[1,8,7,2,64,256]{5,4,2,1,0,3:T(8,128)(2,1)} %all-gather.2.cloned.1.call-done) | data formatting | bytes 7340032 | tf_op jit(solution)/shard_map/all_gather | solution.py:91
  (24 shorter events, 0.6 us)
Async XLA Ops:
  6.5 11.8 %copy-start = (bf16[8,896,128]{2,1,0:T(8,128)(2,1)S(1)}, bf16[8,896,128]{2,1,0:T(8,128)(2,1)}, u32[]{:S(2)}) copy-start(bf16[8,896,128]{2,1,0:T(8,128)(2,1)} %param.5) | copy-start | bytes 5505028
  8.7 19.7 %all-to-all-start = ((s32[8,4,2]{0,1,2:T(4,128)}), s32[8,4,2]{0,1,2:T(4,128)S(1)}, u32[]{:S(2)}, u32[]{:S(2)}) async-start(s32[8,4,2]{0,1,2:T(4,128)} %broadcast_in_dim.55), calls=%async_computation | async-start | bytes 8192 | tf_op jit(solution)/shard_map/all_to_all | solution.py:58
  28.4 5.3 %all-to-all-start.3 = ((bf16[8,4,2,64,128]{4,3,1,0,2:T(8,128)(2,1)}), bf16[8,4,2,64,128]{4,3,1,0,2:T(8,128)(2,1)S(1)}, u32[]{:S(2)}, u32[]{:S(2)}) async-start(bf16[8,4,2,64,128]{4,3,1,0,2:T(8,128)(2,1)} %copy.49), calls=%async_computation.3 | async-start | bytes 2097152 | tf_op jit(solution)/shard_map/all_to_all | solution.py:57
  33.7 5.1 %copy-start.1 = (bf16[8,4,2,64,128]{4,3,1,0,2:T(8,128)(2,1)}, bf16[8,4,2,64,128]{4,3,1,0,2:T(8,128)(2,1)S(1)}, u32[]{:S(2)}) copy-start(bf16[8,4,2,64,128]{4,3,1,0,2:T(8,128)(2,1)S(1)} %all-to-all-done.3) | copy-start | bytes 3145732
  33.7 11.4 %all-to-all-start.1 = ((s32[16,1,1,4]{3,2,1,0:T(1,128)}), s32[16,1,1,4]{3,2,1,0:T(1,128)}, u32[]{:S(2)}, u32[]{:S(2)}) async-start(s32[16,1,1,4]{3,2,1,0:T(1,128)} %copy.43), calls=%async_computation.1 | async-start | bytes 16384 | tf_op jit(solution)/shard_map/all_to_all | solution.py:73
  96.3 10.8 %all-to-all-start.2 = ((s32[1,1,16,4]{3,1,0,2:T(1,128)}), s32[1,1,16,4]{3,1,0,2:T(1,128)S(1)}, u32[]{:S(2)}, u32[]{:S(2)}) async-start(s32[1,1,16,4]{3,1,0,2:T(1,128)} %bitcast.31), calls=%async_computation.2 | async-start | bytes 16384 | tf_op jit(solution)/shard_map/all_to_all | solution.py:72
  100.6 33.3 %all-gather.2.cloned.1.call-start = ((), (), s32[]{:S(2)}) async-start(), calls=%async_computation.6 | async-start | bytes 5505024 | tf_op jit(solution)/shard_map/all_gather | solution.py:91
Sparse Core Ops, SparseCore 0:
  117.2 16.6 all-gather.1
where the time goes:
time: 146 us; the launch traced here: 145 us
  blocking collectives  51.2 us (35%)
  local copies, waits for them, and re-layouts  26.8 us (18%)
  waiting for transfers between devices  24.8 us (17%)
  starting transfers between devices  19.4 us (13%)
  between operations  13.5 us (9%)
  other arithmetic  5.93 us (4%)
  matrix products  3.58 us (2%)
    all_to_all x1, blocking collectives, body(): lax.all_to_all(lax.all_to_all(chosen, 'expert', split_axis=0, concat_axis...  32.6 us
    all_to_all x1, blocking collectives, body(): lax.all_to_all(chosen, 'expert', split_axis=0, concat_axis=2, tiled=True)  18.6 us
    all_gather x1, waiting for transfers between devices, body(): whole_rows = lax.all_gather(owned_rows, 'replica', axis=3, tiled=True)  16.8 us
    all_to_all x1, starting transfers between devices, body(): lax.all_to_all(spots_pair, 'replica', split_axis=2, concat_axis=0, tiled=...  6.41 us
    reshape x1, local copies, waits for them, and re-layouts, body(): placed.reshape(owner_slots, source_count, block_rows, 1, part_rows, owner...  5.3 us
    all_to_all x1, starting transfers between devices, body(): lax.all_to_all(chosen_spots, 'expert', split_axis=0, concat_axis=2, tiled...  5.1 us
    all_to_all x1, waiting for transfers between devices, body(): lax.all_to_all(lax.all_to_all(chosen_spots, 'expert', split_axis=0, conca...  4.42 us
    all_gather x1, local copies, waits for them, and re-layouts, body(): whole_rows = lax.all_gather(owned_rows, 'replica', axis=3, tiled=True)  4.37 us
  transfers between devices with their start and end apart: 5, of which 4 were waited for; matrix products, arithmetic and copies ran while one was open for 14% of the time, Pallas kernels for 0%

commit v1 on v0

--- a/solution.py
+++ b/solution.py
@@ -1,10 +1,20 @@
+import functools
 import math
 import jax
 import jax.numpy as jnp
 from jax import lax
 from jax.sharding import PartitionSpec as P
+from jax.lax import all_gather
 
 BLK = 128
+
+
+def make_the_samples(base_x, pos_dim):
+    res = jnp.concatenate(all_gather(base_x, "replica"), pos_dim)
+    return res
+
+
+_balance_lots_all = functools.partial(make_the_samples, pos_dim=3)
 
 
 def hadamard():
@@ -88,7 +98,7 @@
     placed = jnp.transpose(placed, (0, 1, 3, 5, 2, 4, 6))
     owner_cols = members * block_cols * BLK
     owned_rows = placed.reshape(owner_slots, source_count, block_rows, 1, part_rows, owner_cols)
-    whole_rows = lax.all_gather(owned_rows, "replica", axis=3, tiled=True)
+    whole_rows = _balance_lots_all(owned_rows)
     return whole_rows.reshape(owner_slots, tensor_count * block_rows * BLK, owner_cols)
 
 

time: 146 us -> 146 us (level)
    another operation x0 -> x1, local copies, waits for them, and re-layouts: none -> 5.3 us  [make_the_samples(): res = jnp.concatenate(all_gather(base_x, 'replica'), pos_dim)]
    reshape x1 -> x0, local copies, waits for them, and re-layouts: 5.3 us -> none  [body(): placed.reshape(owner_slots, source_count, block_rows, 1, part_rows, owner...]
where the time goes in v1:
time: 146 us; the launch traced here: 145 us
  blocking collectives  51.2 us (35%)
  local copies, waits for them, and re-layouts  26.8 us (18%)
  waiting for transfers between devices  24.8 us (17%)
  starting transfers between devices  19.4 us (13%)
  between operations  13.5 us (9%)
  other arithmetic  5.93 us (4%)
  matrix products  3.58 us (2%)
    all_to_all x1, blocking collectives, body(): lax.all_to_all(lax.all_to_all(chosen, 'expert', split_axis=0, concat_axis...  32.6 us
    all_to_all x1, blocking collectives, body(): lax.all_to_all(chosen, 'expert', split_axis=0, concat_axis=2, tiled=True)  18.6 us
    all_gather x1, waiting for transfers between devices, make_the_samples(): res = jnp.concatenate(all_gather(base_x, 'replica'), pos_dim)  16.8 us
    all_to_all x1, starting transfers between devices, body(): lax.all_to_all(spots_pair, 'replica', split_axis=2, concat_axis=0, tiled=...  6.41 us
    another operation x1, local copies, waits for them, and re-layouts, make_the_samples(): res = jnp.concatenate(all_gather(base_x, 'replica'), pos_dim)  5.3 us
    all_to_all x1, starting transfers between devices, body(): lax.all_to_all(chosen_spots, 'expert', split_axis=0, concat_axis=2, tiled...  5.1 us
    all_to_all x1, waiting for transfers between devices, body(): lax.all_to_all(lax.all_to_all(chosen_spots, 'expert', split_axis=0, conca...  4.42 us
    all_gather x1, local copies, waits for them, and re-layouts, make_the_samples(): res = jnp.concatenate(all_gather(base_x, 'replica'), pos_dim)  4.37 us
  transfers between devices with their start and end apart: 5, of which 4 were waited for; matrix products, arithmetic and copies ran while one was open for 14% of the time, Pallas kernels for 0%

profile of v1, /device:TPU:1, one launch (start us, length us, event | category | flops | bytes accessed | tf_op | source)
XLA Modules:
  0.0 145.1 jit_solution(11660733728816668597)
XLA Ops:
  6.5 0.9 iota_select_fusion
  7.4 0.7 sort.17
  8.1 0.6 broadcast_in_dim.55
  8.7 6.4 %all-to-all-start = ((s32[8,4,2]{0,1,2:T(4,128)}), s32[8,4,2]{0,1,2:T(4,128)S(1)}, u32[]{:S(2)}, u32[]{:S(2)}) async-start(s32[8,4,2]{0,1,2:T(4,128)} %broadcast_in_dim.55), calls=%async_computation | async-start | bytes 8192 | tf_op jit(solution)/shard_map/all_to_all | solution.py:68
  15.1 0.7 compare_and_fusion
  15.8 0.7 compare_select_fusion.1
  16.4 0.8 copy.38
  17.4 0.7 gather_fusion.4
  18.2 0.1 copy.48
  18.3 0.8 gather_fusion.2
  19.1 4.0 %gather_fusion.1 = f32[32,128,128]{2,1,0:T(8,128)} fusion(f32[8,7,128,1,128]{4,2,1,0,3:T(8,128)} %bitcast.69, s32[32]{0:T(128)S(1)} %reshape.257), kind=kCustom, calls=%fused_computation.1 | custom fusion | bytes 4194688 | tf_op jit(solution)/shard_map/gather | solution.py:52
  23.2 1.9 %convert_subtract_fusion = f32[32,128,128]{2,1,0:T(8,128)S(1)} fusion(f32[32,128,128]{2,1,0:T(8,128)} %gather_fusion.1, bf16[32,128,128]{2,1,0:T(8,128)(2,1)S(1)} %gather_fusion.2), kind=kLoop, calls=%fused_computation.5 | loop fusion | flops 1048576 | bytes 5242880 | tf_op jit(solution)/shard_map/sub | solution.py:59
  25.0 2.3 %fusion.2 = bf16[8,4,128,128]{2,3,1,0:T(8,128)(2,1)S(1)} fusion(f32[8,4,128,128]{3,2,1,0:T(8,128)S(1)} %bitcast.63, pred[8,4]{1,0:T(8,128)(4,1)S(1)} %copy.48, s32[128]{0:T(128)S(1)} %get-tuple-element.7, s32[128]{0:T(128)S(1)} %get-tuple-element.8, s32[128]{0:T(128)S(1)} %get-tuple-element.9, s32[128]{0:T(128)S(1)} %get-tuple-element.10, ...), kind=kOutput, calls=%fused_computation.9 | convolution fusion | flops 806813696 | bytes 3149344 | tf_op jit(solution)/shard_map/ij,pmjk->pmik/dot_general | solution.py:61
  27.3 1.1 copy.49
  28.4 3.6 %all-to-all-start.3 = ((bf16[8,4,2,64,128]{4,3,1,0,2:T(8,128)(2,1)}), bf16[8,4,2,64,128]{4,3,1,0,2:T(8,128)(2,1)S(1)}, u32[]{:S(2)}, u32[]{:S(2)}) async-start(bf16[8,4,2,64,128]{4,3,1,0,2:T(8,128)(2,1)} %copy.49), calls=%async_computation.3 | async-start | bytes 2097152 | tf_op jit(solution)/shard_map/all_to_all | solution.py:67
  32.1 0.6 gather_fusion
  32.7 0.7 copy.43
  33.4 0.3 all-to-all-done.3
  33.7 5.1 %all-to-all-start.1 = ((s32[16,1,1,4]{3,2,1,0:T(1,128)}), s32[16,1,1,4]{3,2,1,0:T(1,128)}, u32[]{:S(2)}, u32[]{:S(2)}) async-start(s32[16,1,1,4]{3,2,1,0:T(1,128)} %copy.43), calls=%async_computation.1 | async-start | bytes 16384 | tf_op jit(solution)/shard_map/all_to_all | solution.py:83
  38.9 2.0 %gather_fusion.3 = bf16[16,4,64,128]{3,2,1,0:T(8,128)(2,1)S(1)} fusion(bf16[16,4,64,128]{3,2,1,0:T(8,128)(2,1)} %bitcast.67, s32[1024]{0:T(1024)S(1)} %pad_clamp_fusion), kind=kCustom, calls=%fused_computation.3 | custom fusion | bytes 2097216 | tf_op jit(solution)/shard_map/jit(_take)/gather | solution.py:70
  40.8 1.1 fusion.5
  42.0 3.2 %all-to-all-done.1 = s32[16,1,1,4]{3,2,1,0:T(1,128)} async-done(((s32[16,1,1,4]{3,2,1,0:T(1,128)}), s32[16,1,1,4]{3,2,1,0:T(1,128)}, u32[]{:S(2)}, u32[]{:S(2)}) %all-to-all-start.1) | async-done | bytes 288 | tf_op jit(solution)/shard_map/all_to_all | solution.py:83
  45.2 18.6 %all_to_all.78 = bf16[16,1,1,4,64,128]{5,4,3,2,1,0:T(8,128)(2,1)S(1)} all-to-all(bf16[16,1,1,4,64,128]{5,4,3,2,1,0:T(8,128)(2,1)} %fusion.5), channel_id=1, replica_groups=mesh['expert'=16,'tensor'=8,'replica'=2] {'expert'}, dimensions={0} | all-to-all | bytes 2097152 | tf_op jit(solution)/shard_map/all_to_all | solution.py:76
  63.8 32.6 %all_to_all.79 = bf16[1,1,16,4,64,128]{5,4,3,1,0,2:T(8,128)(2,1)} all-to-all(bf16[1,1,16,4,64,128]{5,4,3,1,0,2:T(8,128)(2,1)S(1)} %bitcast.68), channel_id=1, replica_groups=mesh['expert'=16,'tensor'=8,'replica'=2] {'tensor'}, dimensions={2} | all-to-all | bytes 2097152 | tf_op jit(solution)/shard_map/all_to_all | solution.py:75
  96.3 4.3 %all-to-all-start.2 = ((s32[1,1,16,4]{3,1,0,2:T(1,128)}), s32[1,1,16,4]{3,1,0,2:T(1,128)S(1)}, u32[]{:S(2)}, u32[]{:S(2)}) async-start(s32[1,1,16,4]{3,1,0,2:T(1,128)} %bitcast.32), calls=%async_computation.2 | async-start | bytes 16384 | tf_op jit(solution)/shard_map/all_to_all | solution.py:82
  100.7 2.1 %copy.52 = bf16[1,1,16,4,64,128]{5,3,4,2,1,0:T(4,128)(2,1)S(1)} copy(bf16[1,1,16,4,64,128]{5,4,3,1,0,2:T(8,128)(2,1)} %all_to_all.79) | data formatting | bytes 2097152 | tf_op jit(solution)/shard_map/all_to_all | solution.py:75
  102.8 4.4 %all-to-all-done.2 = s32[1,1,16,4]{3,1,0,2:T(1,128)S(1)} async-done(((s32[1,1,16,4]{3,1,0,2:T(1,128)}), s32[1,1,16,4]{3,1,0,2:T(1,128)S(1)}, u32[]{:S(2)}, u32[]{:S(2)}) %all-to-all-start.2) | async-done | bytes 288 | tf_op jit(solution)/shard_map/all_to_all | solution.py:82
  107.2 1.3 convert_bitcast_fusion
  108.5 3.3 %copy.53 = bf16[1,8,7,64,2,1,128]{6,4,3,2,1,5,0:T(2,128)(2,1)} copy(bf16[1,8,7,64,2,1,128]{6,2,3,4,1,5,0:T(8,128)(2,1)S(1)} %convert_bitcast_fusion) | data formatting | bytes 3670016 | tf_op jit(solution)/shard_map/transpose | solution.py:98
  111.8 5.3 %all_gather_reshape.3 = bf16[1,1,8,7,1,64,256]{6,5,3,2,4,1,0:T(8,128)(2,1)} reshape(bf16[1,8,7,64,2,1,128]{6,4,3,2,1,5,0:T(2,128)(2,1)} %copy.53) | data formatting | bytes 3670016 | tf_op jit(solution)/shard_map/all_gather;reshape | solution.py:13
  117.1 16.8 %all-gather.2.cloned.1.call-done = bf16[2,1,8,7,1,64,256]{6,5,4,3,2,1,0:T(8,128)(2,1)} async-done(((bf16[1,1,8,7,1,64,256]{6,5,4,3,2,1,0:T(8,128)(2,1)}), bf16[2,1,8,7,1,64,256]{6,5,4,3,2,1,0:T(8,128)(2,1)}) %all-gather.2.cloned.1.call-update) | async-done | bytes 3670032 | tf_op jit(solution)/shard_map/all_gather | solution.py:13
  133.9 4.4 %copy.55 = bf16[2,1,8,7,1,64,256]{6,5,0,3,2,4,1:T(8,128)(2,1)} copy(bf16[2,1,8,7,1,64,256]{6,5,4,3,2,1,0:T(8,128)(2,1)} %all-gather.2.cloned.1.call-done) | data formatting | bytes 7340032 | tf_op jit(solution)/shard_map/all_gather | solution.py:13
  (24 shorter events, 0.6 us)
Async XLA Ops:
  6.5 11.8 %copy-start = (bf16[8,896,128]{2,1,0:T(8,128)(2,1)S(1)}, bf16[8,896,128]{2,1,0:T(8,128)(2,1)}, u32[]{:S(2)}) copy-start(bf16[8,896,128]{2,1,0:T(8,128)(2,1)} %param.5) | copy-start | bytes 5505028
  8.7 19.7 %all-to-all-start = ((s32[8,4,2]{0,1,2:T(4,128)}), s32[8,4,2]{0,1,2:T(4,128)S(1)}, u32[]{:S(2)}, u32[]{:S(2)}) async-start(s32[8,4,2]{0,1,2:T(4,128)} %broadcast_in_dim.55), calls=%async_computation | async-start | bytes 8192 | tf_op jit(solution)/shard_map/all_to_all | solution.py:68
  28.4 5.3 %all-to-all-start.3 = ((bf16[8,4,2,64,128]{4,3,1,0,2:T(8,128)(2,1)}), bf16[8,4,2,64,128]{4,3,1,0,2:T(8,128)(2,1)S(1)}, u32[]{:S(2)}, u32[]{:S(2)}) async-start(bf16[8,4,2,64,128]{4,3,1,0,2:T(8,128)(2,1)} %copy.49), calls=%async_computation.3 | async-start | bytes 2097152 | tf_op jit(solution)/shard_map/all_to_all | solution.py:67
  33.7 5.1 %copy-start.1 = (bf16[8,4,2,64,128]{4,3,1,0,2:T(8,128)(2,1)}, bf16[8,4,2,64,128]{4,3,1,0,2:T(8,128)(2,1)S(1)}, u32[]{:S(2)}) copy-start(bf16[8,4,2,64,128]{4,3,1,0,2:T(8,128)(2,1)S(1)} %all-to-all-done.3) | copy-start | bytes 3145732
  33.7 11.4 %all-to-all-start.1 = ((s32[16,1,1,4]{3,2,1,0:T(1,128)}), s32[16,1,1,4]{3,2,1,0:T(1,128)}, u32[]{:S(2)}, u32[]{:S(2)}) async-start(s32[16,1,1,4]{3,2,1,0:T(1,128)} %copy.43), calls=%async_computation.1 | async-start | bytes 16384 | tf_op jit(solution)/shard_map/all_to_all | solution.py:83
  96.3 10.8 %all-to-all-start.2 = ((s32[1,1,16,4]{3,1,0,2:T(1,128)}), s32[1,1,16,4]{3,1,0,2:T(1,128)S(1)}, u32[]{:S(2)}, u32[]{:S(2)}) async-start(s32[1,1,16,4]{3,1,0,2:T(1,128)} %bitcast.32), calls=%async_computation.2 | async-start | bytes 16384 | tf_op jit(solution)/shard_map/all_to_all | solution.py:82
  100.6 33.3 %all-gather.2.cloned.1.call-start = ((), (), s32[]{:S(2)}) async-start(), calls=%async_computation.6 | async-start | bytes 5505024 | tf_op jit(solution)/shard_map/all_gather | solution.py:13
Sparse Core Ops, SparseCore 0:
  117.2 16.6 all-gather.1
